TPU v7x, 32 devices: a whole 2x2x4 slice. The times are simulated.
32 devices in a mesh: path: 4 (over z), tm: 8 (over y, x, core).
Axes of the slice: x: 2, y: 2, z: 4, core: 2. Of those that a mesh axis runs over, the one named last changes fastest.
Arguments:
- values: bfloat16 [2048, 16, 2048], P('path', 'tm'), may hold values from -5 to 5
- hazard: float32 [16, 2048], P('tm', 'path'), may hold values from 0.0125 to 0.1875
- spread: float32 [16], P('tm'), may hold values from 0.3 to 3
- trade_set: int32 [2048], replicated, may hold values from 0 to 255
Outputs:
- pathwise_fva: float32 [2048, 256], P(('path', 'tm'))
- set_fva: float32 [256], P(('path', 'tm'))
All inputs are finite; a program needn't handle non-finite values.
Results may differ from a plain program's by a relative error of at most 0.0003.
Values sent between devices are 32-bit elements; how exact they have to be, the bound alone decides.
A program may use at most 64 MiB of HBM per device.

v0:
```python
import jax
import jax.numpy as jnp
from jax import lax
from jax.sharding import PartitionSpec as P

SETS = 256


def on_device(values, hazard, spread, trade_set):
    paths_dev, dates_dev, trades = values.shape
    dates_total = dates_dev * lax.axis_size("tm")
    paths_total = paths_dev * lax.axis_size("path")
    onehot = (trade_set[:, None] == jnp.arange(SETS, dtype=jnp.int32)[None, :]).astype(jnp.bfloat16)
    netted = jnp.dot(
        values.reshape(paths_dev * dates_dev, trades), onehot, preferred_element_type=jnp.float32
    )
    positive = jnp.maximum(netted.reshape(paths_dev, dates_dev, SETS), 0.0)
    survival = jnp.exp(-jnp.cumsum(hazard, axis=0))
    block_product = survival[-1]
    weights = jnp.transpose(spread[:, None] * survival)
    local_sum = jnp.einsum("pt,pts->ps", weights, positive, precision=lax.Precision.HIGHEST)
    gathered_sums, gathered_products = (
        lax.all_to_all(local_sum[None], "tm", split_axis=1, concat_axis=0, tiled=True),
        lax.all_to_all(block_product[None], "tm", split_axis=1, concat_axis=0, tiled=True),
    )
    earlier = jnp.concatenate(
        [jnp.ones_like(gathered_products[:1]), jnp.cumprod(gathered_products[:-1], axis=0)], axis=0
    )
    shares = jnp.einsum("kp,kps->ps", earlier, gathered_sums, precision=lax.Precision.HIGHEST)
    pathwise_fva = shares / dates_total
    set_part = jnp.sum(pathwise_fva, axis=0) / paths_total
    set_fva = lax.psum_scatter(set_part, ("path", "tm"), scatter_dimension=0, tiled=True)
    return (pathwise_fva, set_fva)


def solution(mesh):
    in_specs = (P("path", "tm", None), P("tm", "path"), P("tm"), P())
    out_specs = (P(("path", "tm"), None), P(("path", "tm")))
    return jax.shard_map(
        on_device, mesh=mesh, in_specs=in_specs, out_specs=out_specs, check_vma=False
    )
```

profile of v0, /device:TPU:0, one launch (start us, length us, event | category | flops | bytes accessed | tf_op | source)
XLA Modules:
  0.0 80.7 jit_solution(11877485971977223632)
XLA Ops:
  0.6 0.7 reduce_window_sum.11
  1.3 0.7 multiply_bitcast_fusion
  2.1 0.7 all_to_all.9
  2.8 5.2 %all-to-all-start = ((f32[1,8,64]{2,0,1:T(1,128)}), f32[1,8,64]{2,0,1:T(1,128)S(1)}, u32[]{:S(2)}, u32[]{:S(2)}) async-start(f32[1,8,64]{2,0,1:T(1,128)} %all_to_all.9), calls=%async_computation | async-start | bytes 8192 | tf_op jit(solution)/shard_map/all_to_all | solution.py:24
  8.0 0.1 copy.8
  8.1 0.0 copy-start
  8.1 7.2 %reshape.21 = bf16[1024,2048]{1,0:T(8,128)(2,1)} reshape(bf16[512,2,2048]{2,1,0:T(2,128)(2,1)} %param.4) | data formatting | bytes 8388608 | tf_op jit(solution)/shard_map/reshape | solution.py:15
  15.4 0.0 copy-done
  15.4 3.8 %fusion.1 = f32[1024,256]{0,1:T(8,128)S(1)} fusion(bf16[1024,2048]{1,0:T(8,128)(2,1)} %reshape.21, s32[2048]{0:T(1024)S(1)} %copy-done), kind=kOutput, calls=%fused_computation.3 | convolution fusion | flops 1075052544 | bytes 5251072 | tf_op jit(solution)/shard_map/dot_general | solution.py:14
  19.2 0.3 copy.7
  19.6 0.6 max.15
  20.2 3.8 %fusion.7 = f32[512,1,256]{2,1,0:T(1,128)S(1)} fusion(f32[512,2,1]{1,2,0:T(1,128)S(1)} %copy.8, f32[512,2,256]{2,1,0:T(2,128)S(1)} %max.15), kind=kOutput, calls=%fused_computation.16 | convolution fusion | flops 3145728 | bytes 1576960 | tf_op jit(solution)/shard_map/pt,pts->ps/dot_general | solution.py:21
  24.1 1.1 %broadcast_in_dim.2 = f32[1,512,256]{2,0,1:T(1,128)} reshape(f32[512,256]{1,0:T(8,128)S(1)} %bitcast.23) | data formatting | bytes 1048576 | tf_op jit(solution)/shard_map/broadcast_in_dim | solution.py:23
  25.2 0.0 all-to-all-done
  25.2 4.2 %all-to-all-start.1 = ((f32[1,512,256]{2,0,1:T(1,128)}), f32[1,512,256]{2,0,1:T(1,128)S(1)}, u32[]{:S(2)}, u32[]{:S(2)}) async-start(f32[1,512,256]{2,0,1:T(1,128)} %broadcast_in_dim.2), calls=%async_computation.1 | async-start | bytes 1048576 | tf_op jit(solution)/shard_map/all_to_all | solution.py:23
  29.5 0.1 copy.10
  29.6 9.6 %all-to-all-done.1 = f32[1,512,256]{2,0,1:T(1,128)S(1)} async-done(((f32[1,512,256]{2,0,1:T(1,128)}), f32[1,512,256]{2,0,1:T(1,128)S(1)}, u32[]{:S(2)}, u32[]{:S(2)}) %all-to-all-start.1) | async-done | bytes 524320 | tf_op jit(solution)/shard_map/all_to_all | solution.py:23
  39.2 0.9 %fusion.4 = f32[64,1,256]{2,1,0:T(1,128)S(1)} fusion(f32[8,64,1]{0,2,1:T(1,128)S(1)} %copy.10, f32[8,64,256]{2,1,0:T(8,128)S(1)} %bitcast.22), kind=kOutput, calls=%fused_computation.5 | convolution fusion | flops 1572864 | bytes 591872 | tf_op jit(solution)/shard_map/kp,kps->ps/dot_general | solution.py:29
  40.0 0.6 fusion.6
  40.7 39.4 %all-reduce.1 = f32[256]{0:T(256)S(1)} all-reduce(f32[256]{0:T(256)S(1)} %broadcast_multiply_fusion), channel_id=2, replica_groups=mesh['path'=4,'tm'=8] {'path','tm'}, use_global_device_ids=true, to_apply=%region_3.4.clone | all-reduce | flops 256 | bytes 2048
  80.1 0.6 dynamic-slice
  (8 shorter events, 0.1 us)
Async XLA Ops:
  2.8 22.5 %all-to-all-start = ((f32[1,8,64]{2,0,1:T(1,128)}), f32[1,8,64]{2,0,1:T(1,128)S(1)}, u32[]{:S(2)}, u32[]{:S(2)}) async-start(f32[1,8,64]{2,0,1:T(1,128)} %all_to_all.9), calls=%async_computation | async-start | bytes 8192 | tf_op jit(solution)/shard_map/all_to_all | solution.py:24
  8.1 7.2 %copy-start = (s32[2048]{0:T(1024)S(1)}, s32[2048]{0:T(1024)}, u32[]{:S(2)}) copy-start(s32[2048]{0:T(1024)} %param.7) | copy-start | bytes 24580
  25.2 13.9 %all-to-all-start.1 = ((f32[1,512,256]{2,0,1:T(1,128)}), f32[1,512,256]{2,0,1:T(1,128)S(1)}, u32[]{:S(2)}, u32[]{:S(2)}) async-start(f32[1,512,256]{2,0,1:T(1,128)} %broadcast_in_dim.2), calls=%async_computation.1 | async-start | bytes 1048576 | tf_op jit(solution)/shard_map/all_to_all | solution.py:23
where the time goes:
time: 81.2 us; the launch traced here: 80.7 us
  blocking collectives  39.4 us (49%)
  local copies, waits for them, and re-layouts  10.9 us (13%)
  waiting for transfers between devices  9.58 us (12%)
  starting transfers between devices  9.4 us (12%)
  matrix products  8.55 us (11%)
  other arithmetic  2.11 us (3%)
    unnamed x1, blocking collectives  39.4 us
    all_to_all x1, waiting for transfers between devices, on_device(): lax.all_to_all(local_sum[None], 'tm', split_axis=1, concat_axis=0, tiled=...  9.57 us
    reshape x1, local copies, waits for them, and re-layouts, on_device(): values.reshape(paths_dev * dates_dev, trades)  7.22 us
    all_to_all x1, starting transfers between devices, on_device(): lax.all_to_all(block_product[None], 'tm', split_axis=1, concat_axis=0, ti...  5.2 us
    all_to_all x1, starting transfers between devices, on_device(): lax.all_to_all(local_sum[None], 'tm', split_axis=1, concat_axis=0, tiled=...  4.2 us
    dot_general x1, matrix products, on_device(): jnp.dot(values.reshape(paths_dev * dates_dev, trades), onehot, preferred_...  3.85 us
    dot_general x1, matrix products, on_device(): jnp.einsum('pt,pts->ps', weights, positive, precision=lax.Precision.HIGHEST)  3.85 us
  transfers between devices with their start and end apart: 2, of which 1 were waited for; matrix products, arithmetic and copies ran while one was open for 21% of the time, Pallas kernels for 0%

commit v1 on v0

v1 whole, which is shorter than its diff:
```python
import functools

import jax
import jax.numpy as jnp
from jax import lax
from jax.experimental import pallas as pl
from jax.experimental.pallas import tpu as pltpu
from jax.sharding import PartitionSpec as P

SETS = 256
CHUNK_PATHS = 128
LANES = 128
MESH = pl.DeviceIdType.MESH


def kernel(
    n_path, n_tm, values, hazard_in, spread, trade_in, out, set_out,
    vbuf, ts, oh, hz, nbuf, wt, contrib, recv, hbuf, erow, ecol, setrow, setbuf,
    load_sem, small_sem, h_send, h_recv, b_send, b_recv, s_send, s_recv,
):
    paths, dates, trades = values.shape
    own = paths // n_tm
    chunks = paths // CHUNK_PATHS
    per = n_tm // chunks
    n_all = n_path * n_tm
    path_at, me = lax.axis_index("path"), lax.axis_index("tm")
    flat = path_at * n_tm + me
    rows = CHUNK_PATHS * dates
    my_chunk = lax.div(me, per)
    first = [lax.rem(my_chunk + 1 + i, chunks) for i in range(chunks)]
    flat_values = values.reshape(paths * dates, trades)

    def load(i):
        span = pl.ds(pl.multiple_of(first[i] * rows, rows), rows)
        return pltpu.make_async_copy(flat_values.at[span], vbuf.at[span], load_sem.at[i])

    copy_trades = pltpu.make_async_copy(trade_in, ts, small_sem.at[0])
    copy_hazard = pltpu.make_async_copy(hazard_in, hz, small_sem.at[1])
    copy_trades.start()
    copy_hazard.start()
    for i in range(chunks):
        load(i).start()

    barrier = pltpu.get_barrier_semaphore()

    def greet(k, carry):
        other = lax.rem(flat + k, n_all)
        pl.semaphore_signal(
            barrier, inc=1, device_id=(lax.div(other, n_tm), lax.rem(other, n_tm)), device_id_type=MESH
        )
        return carry

    lax.fori_loop(1, n_all, greet, 0)

    copy_trades.wait()
    set_at = lax.broadcasted_iota(jnp.int32, (SETS, LANES), 0)
    for block in range(trades // LANES):
        same = jnp.broadcast_to(ts[pl.ds(block, 1), :], (SETS, LANES)) == set_at
        oh[:, pl.ds(block * LANES, LANES)] = jnp.where(same, 1.0, 0.0).astype(jnp.bfloat16)

    copy_hazard.wait()
    total = jnp.zeros((1, paths), jnp.float32)
    weight_rows = []
    scale = 1.0 / (dates * n_tm)
    for d in range(dates):
        total = total + hz[pl.ds(d, 1), :]
        weight_rows.append((spread[d] * scale) * jnp.exp(-total))
    weight_rows.append(jnp.zeros((8 - dates, paths), jnp.float32))
    wt[...] = jnp.transpose(jnp.concatenate(weight_rows, axis=0))
    hbuf[me] = hz[...]

    def hazard_copy(other):
        return pltpu.make_async_remote_copy(
            src_ref=hz, dst_ref=hbuf.at[me], send_sem=h_send.at[other], recv_sem=h_recv.at[me],
            device_id=(path_at, other), device_id_type=MESH,
        )

    def hazard_arrival(other):
        return pltpu.make_async_remote_copy(
            src_ref=hz, dst_ref=hbuf.at[other], send_sem=h_send.at[other], recv_sem=h_recv.at[other],
            device_id=(path_at, other), device_id_type=MESH,
        )

    def own_rows(index):
        return pl.ds(pl.multiple_of(index * own, own), own)

    def block_copy(other):
        return pltpu.make_async_remote_copy(
            src_ref=contrib.at[own_rows(other)], dst_ref=recv.at[me],
            send_sem=b_send.at[other], recv_sem=b_recv.at[me],
            device_id=(path_at, other), device_id_type=MESH,
        )

    def block_arrival(other):
        return pltpu.make_async_remote_copy(
            src_ref=contrib.at[own_rows(other)], dst_ref=recv.at[other],
            send_sem=b_send.at[other], recv_sem=b_recv.at[other],
            device_id=(path_at, other), device_id_type=MESH,
        )

    peers = [lax.rem(me + k, n_tm) for k in range(1, n_tm)]
    for i in range(chunks):
        load(i).wait()
        span = pl.ds(pl.multiple_of(first[i] * rows, rows), rows)
        netted = lax.dot_general(
            vbuf[span, :], oh[...], (((1,), (1,)), ((), ())), preferred_element_type=jnp.float32
        )
        for h in range(SETS // LANES):
            nbuf[i, h] = netted[:, h * LANES : (h + 1) * LANES]
        path_span = pl.ds(pl.multiple_of(first[i] * CHUNK_PATHS, CHUNK_PATHS), CHUNK_PATHS)
        weight = wt[path_span, :]
        for h in range(SETS // LANES):
            part = None
            for d in range(dates):
                picked = nbuf[i, h, pl.ds(d, CHUNK_PATHS, stride=dates), :]
                term = weight[:, d : d + 1] * jnp.maximum(picked, 0.0)
                part = term if part is None else part + term
            contrib[path_span, pl.ds(h * LANES, LANES)] = part
        if i == 0:
            pl.semaphore_wait(barrier, n_all - 1)
            for other in peers:
                hazard_copy(other).start()
        if i < chunks - 1:
            for q in range(per):
                block_copy(first[i] * per + q).start()
        else:
            for q in range(1, per):
                block_copy(my_chunk * per + lax.rem(lax.rem(me, per) + q, per)).start()

    for other in peers:
        hazard_arrival(other).wait_recv()
    block_sums = jnp.sum(hbuf[...], axis=1)
    before = jnp.zeros((1, paths), jnp.float32)
    prefix = []
    for k in range(n_tm):
        prefix.append(before)
        before = before + block_sums[k : k + 1, :]
    earlier = jnp.exp(-jnp.concatenate(prefix, axis=0))
    erow[...] = earlier
    ecol[...] = jnp.transpose(earlier)
    mine = jnp.broadcast_to(erow[pl.ds(me, 1), :], (8, paths))
    set_part = jnp.dot(
        mine, contrib[...], precision=lax.Precision.HIGHEST, preferred_element_type=jnp.float32
    )
    setrow[...] = set_part[:1] * (1.0 / (paths * n_path))

    def set_copy(k, arrival):
        other = lax.rem(flat + k, n_all)
        slot = other if arrival else flat
        return pltpu.make_async_remote_copy(
            src_ref=setrow, dst_ref=setbuf.at[slot], send_sem=s_send.at[other], recv_sem=s_recv.at[slot],
            device_id=(lax.div(other, n_tm), lax.rem(other, n_tm)), device_id_type=MESH,
        )

    def send_set(k, carry):
        set_copy(k, False).start()
        return carry

    lax.fori_loop(1, n_all, send_set, 0)
    setbuf[flat] = setrow[...]

    recv[me] = contrib[own_rows(me), :]
    for other in peers:
        block_arrival(other).wait_recv()
    factor = ecol[own_rows(me), :]
    result = None
    for k in range(n_tm):
        term = factor[:, k : k + 1] * recv[k]
        result = term if result is None else result + term
    out[...] = result

    def take_set(k, carry):
        set_copy(k, True).wait_recv()
        return carry

    lax.fori_loop(1, n_all, take_set, 0)
    sums = jnp.broadcast_to(jnp.sum(setbuf[...], axis=0), (8, SETS))
    share = SETS // n_all
    turned = pltpu.roll(sums, lax.rem(SETS - flat * share, SETS), 1)
    set_out[...] = turned[:1, :share]

    for other in peers:
        hazard_copy(other).wait_send()
        block_copy(other).wait_send()

    def drain(k, carry):
        set_copy(k, False).wait_send()
        return carry

    lax.fori_loop(1, n_all, drain, 0)


def solution(mesh):
    n_path, n_tm = mesh.shape["path"], mesh.shape["tm"]
    n_all = n_path * n_tm

    def on_device(values, hazard, spread, trade_set):
        paths, dates, trades = values.shape
        own = paths // n_tm
        chunks = paths // CHUNK_PATHS
        f32 = jnp.float32
        any_space = pl.BlockSpec(memory_space=pltpu.HBM)
        vmem = pl.BlockSpec(memory_space=pltpu.VMEM)
        dma = pltpu.SemaphoreType.DMA
        pathwise, sets = pl.pallas_call(
            functools.partial(kernel, n_path, n_tm),
            out_shape=(
                jax.ShapeDtypeStruct((own, SETS), f32),
                jax.ShapeDtypeStruct((1, SETS // n_all), f32),
            ),
            in_specs=[any_space, any_space, pl.BlockSpec(memory_space=pltpu.SMEM), any_space],
            out_specs=(vmem, vmem),
            scratch_shapes=[
                pltpu.VMEM((paths * dates, trades), jnp.bfloat16),
                pltpu.VMEM((trades // LANES, LANES), jnp.int32),
                pltpu.VMEM((SETS, trades), jnp.bfloat16),
                pltpu.VMEM((dates, paths), f32),
                pltpu.VMEM((chunks, SETS // LANES, CHUNK_PATHS * dates, LANES), f32),
                pltpu.VMEM((paths, 8), f32),
                pltpu.VMEM((paths, SETS), f32),
                pltpu.VMEM((n_tm, own, SETS), f32),
                pltpu.VMEM((n_tm, dates, paths), f32),
                pltpu.VMEM((n_tm, paths), f32),
                pltpu.VMEM((paths, n_tm), f32),
                pltpu.VMEM((1, SETS), f32),
                pltpu.VMEM((n_all, 1, SETS), f32),
                dma((chunks,)),
                dma((2,)),
                dma((n_tm,)),
                dma((n_tm,)),
                dma((n_tm,)),
                dma((n_tm,)),
                dma((n_all,)),
                dma((n_all,)),
            ],
            compiler_params=pltpu.CompilerParams(
                collective_id=0, has_side_effects=True, vmem_limit_bytes=63 * 1024 * 1024
            ),
        )(values, hazard, spread, trade_set.reshape(trades // LANES, LANES))
        return pathwise, sets.reshape(SETS // n_all)

    in_specs = (P("path", "tm", None), P("tm", "path"), P("tm"), P())
    out_specs = (P(("path", "tm"), None), P(("path", "tm")))
    return jax.shard_map(
        on_device, mesh=mesh, in_specs=in_specs, out_specs=out_specs, check_vma=False
    )
```

time: 81.2 us -> 21.3 us (0.26)
  blocking collectives: 39.4 us -> 0 us
  Pallas kernels: 0 us -> 17.9 us
  waiting for transfers between devices: 9.58 us -> 0 us
  starting transfers between devices: 9.4 us -> 0 us
  matrix products: 8.55 us -> 0 us
  local copies, waits for them, and re-layouts: 10.9 us -> 2.59 us
  other arithmetic: 2.11 us -> 0 us
    unnamed x1 -> x0, blocking collectives: 39.4 us -> none
    pallas_call x0 -> x1, Pallas kernels: none -> 17.9 us  [on_device(): pl.pallas_call(functools.partial(kernel, n_path, n_tm), out_shape=(jax.Sh...]
    all_to_all x2 -> x0, waiting for transfers between devices: 9.58 us -> none  [the longest x1 9.57 us: on_device(): lax.all_to_all(local_sum[None], 'tm', split_axis=1, concat_axis=0, tiled=...]
    all_to_all x2 -> x0, starting transfers between devices: 9.4 us -> none  [the longest x1 5.2 us: on_device(): lax.all_to_all(block_product[None], 'tm', split_axis=1, concat_axis=0, ti...]
    dot_general x3 -> x0, matrix products: 8.55 us -> none  [the longest x1 3.85 us: on_device(): jnp.dot(values.reshape(paths_dev * dates_dev, trades), onehot, preferred_...]
    reshape x1 -> x0, local copies, waits for them, and re-layouts: 7.22 us -> none  [on_device(): values.reshape(paths_dev * dates_dev, trades)]
    unnamed x5 -> x2, local copies, waits for them, and re-layouts: 0.63 us -> 2.59 us
    broadcast_in_dim x1 -> x0, local copies, waits for them, and re-layouts: 1.15 us -> none  [on_device(): local_sum[None]]
  transfers between devices with their start and end apart: 2 -> 0, of which waited for: 1 -> 0; matrix products, arithmetic and copies ran while one was open for 21% -> 0% of each run, Pallas kernels for 0% -> 0%
where the time goes in v1:
time: 21.3 us; the launch traced here: 21.1 us
  Pallas kernels  17.9 us (84%)
  local copies, waits for them, and re-layouts  2.59 us (12%)
  between operations  0.64 us (3%)
    pallas_call x1, Pallas kernels, on_device(): pl.pallas_call(functools.partial(kernel, n_path, n_tm), out_shape=(jax.Sh...  17.9 us
    unnamed x2, local copies, waits for them, and re-layouts  2.59 us

profile of v1, /device:TPU:0, one launch (start us, length us, event | category | flops | bytes accessed | tf_op | source)
XLA Modules:
  0.0 21.1 jit_solution(1725470936446189472)
XLA Ops:
  0.6 17.9 %shard_map.59 = (f32[64,256]{1,0:T(8,128)}, f32[1,8]{1,0:T(1,128)}) custom-call(bf16[512,2,2048]{2,1,0:T(2,128)(2,1)} %values.1, f32[2,512]{1,0:T(2,128)} %hazard_in.1, f32[2]{0:T(128)} %spread.1, s32[16,128]{1,0:T(8,128)} %bitcast.2), custom_call_target="tpu_custom_call" | custom-call | tf_op jit(solution)/shard_map/pallas_call | solution.py:205
  18.5 1.5 %copy.8 = f32[64,256]{1,0:T(8,128)} copy(f32[64,256]{1,0:T(8,128)} %get-tuple-element.8) | data formatting | bytes 131072
  20.0 1.1 %copy.9 = f32[8]{0:T(128)} copy(f32[8]{0:T(128)} %bitcast.3) | data formatting | bytes 64

commit v2 on v1

v2 whole, which is shorter than its diff:
```python
import functools

import jax
import jax.numpy as jnp
from jax import lax
from jax.experimental import pallas as pl
from jax.experimental.pallas import tpu as pltpu
from jax.sharding import PartitionSpec as P

SETS = 256
CHUNK_PATHS = 128
LANES = 128
MESH = pl.DeviceIdType.MESH


def kernel(
    n_path, n_tm, values, hazard_in, spread, trade_in, out, set_out,
    vbuf, ts, oh, hz, nbuf, wt, contrib, pair, comb, recv, hbuf, pcol, erow, ecol, row_a, row_b, rows_a, rows_b,
    load_sem, small_sem, h_send, h_recv, p_send, p_recv, b_send, b_recv, a_send, a_recv, z_send, z_recv,
):
    paths, dates, trades = values.shape
    own = paths // n_tm
    chunks = paths // CHUNK_PATHS
    per = n_tm // chunks
    n_all = n_path * n_tm
    chips = n_tm // 2
    path_at, me = lax.axis_index("path"), lax.axis_index("tm")
    flat = path_at * n_tm + me
    chip, core = lax.div(me, 2), lax.rem(me, 2)
    partner = me + 1 - 2 * core
    peers = [lax.rem(me + k, n_tm) for k in range(1, n_tm)]
    path_peers = [lax.rem(path_at + k, n_path) for k in range(1, n_path)]
    rows = CHUNK_PATHS * dates
    my_chunk = lax.div(me, per)
    first = [lax.rem(my_chunk + 1 + i, chunks) for i in range(chunks)]
    flat_values = values.reshape(paths * dates, trades)

    def load(i):
        span = pl.ds(pl.multiple_of(first[i] * rows, rows), rows)
        return pltpu.make_async_copy(flat_values.at[span], vbuf.at[span], load_sem.at[i])

    copy_trades = pltpu.make_async_copy(trade_in, ts, small_sem.at[0])
    copy_hazard = pltpu.make_async_copy(hazard_in, hz, small_sem.at[1])
    copy_trades.start()
    copy_hazard.start()
    for i in range(chunks):
        load(i).start()

    barrier = pltpu.get_barrier_semaphore()

    for other in peers:
        pl.semaphore_signal(barrier, inc=1, device_id=(path_at, other), device_id_type=MESH)
    for other in path_peers:
        pl.semaphore_signal(barrier, inc=1, device_id=(other, me), device_id_type=MESH)

    copy_trades.wait()
    set_at = lax.broadcasted_iota(jnp.int32, (SETS, LANES), 0)
    for block in range(trades // LANES):
        same = jnp.broadcast_to(ts[pl.ds(block, 1), :], (SETS, LANES)) == set_at
        oh[:, pl.ds(block * LANES, LANES)] = jnp.where(same, 1.0, 0.0).astype(jnp.bfloat16)

    copy_hazard.wait()
    total = jnp.zeros((1, paths), jnp.float32)
    weight_rows = []
    scale = 1.0 / (dates * n_tm)
    for d in range(dates):
        total = total + hz[pl.ds(d, 1), :]
        weight_rows.append((spread[d] * scale) * jnp.exp(-total))
    weight_rows.append(jnp.zeros((8 - dates, paths), jnp.float32))
    wt[...] = jnp.transpose(jnp.concatenate(weight_rows, axis=0))
    hbuf[me] = hz[...]

    def remote(src, dst, send, recv_at, device):
        return pltpu.make_async_remote_copy(
            src_ref=src, dst_ref=dst, send_sem=send, recv_sem=recv_at, device_id=device, device_id_type=MESH
        )

    def own_rows(index):
        return pl.ds(pl.multiple_of(index * own, own), own)

    def hazard_copy(other, slot):
        return remote(hz, hbuf.at[slot], h_send.at[other], h_recv.at[slot], (path_at, other))

    def pair_copy(q):
        theirs = contrib.at[own_rows(q * 2 + 1 - core)]
        return remote(theirs, pair.at[q], p_send.at[q], p_recv.at[q], (path_at, partner))

    def block_copy(q, slot):
        return remote(comb.at[q], recv.at[slot], b_send.at[q], b_recv.at[slot], (path_at, q * 2 + core))

    def plane_row(other, slot):
        return remote(row_a, rows_a.at[slot], a_send.at[other], a_recv.at[slot], (path_at, other))

    def path_row(other, slot):
        return remote(row_b, rows_b.at[slot], z_send.at[other], z_recv.at[slot], (other, me))

    def combine(q):
        pair_copy(q).wait_recv()
        mine = own_rows(q * 2 + core)
        factor = pcol[mine, :]
        return factor[:, 0:1] * contrib[mine, :] + factor[:, 1:2] * pair[q]

    def forward(i):
        for k in range(per // 2):
            q = first[i] * (per // 2) + k
            comb[q] = combine(q)
            block_copy(q, chip).start()

    for i in range(chunks):
        load(i).wait()
        span = pl.ds(pl.multiple_of(first[i] * rows, rows), rows)
        netted = lax.dot_general(
            vbuf[span, :], oh[...], (((1,), (1,)), ((), ())), preferred_element_type=jnp.float32
        )
        for h in range(SETS // LANES):
            nbuf[i, h] = netted[:, h * LANES : (h + 1) * LANES]
        path_span = pl.ds(pl.multiple_of(first[i] * CHUNK_PATHS, CHUNK_PATHS), CHUNK_PATHS)
        weight = wt[path_span, :]
        for h in range(SETS // LANES):
            part = None
            for d in range(dates):
                picked = nbuf[i, h, pl.ds(d, CHUNK_PATHS, stride=dates), :]
                term = weight[:, d : d + 1] * jnp.maximum(picked, 0.0)
                part = term if part is None else part + term
            contrib[path_span, pl.ds(h * LANES, LANES)] = part
        if i == 0:
            pl.semaphore_wait(barrier, n_tm - 1 + n_path - 1)
            hazard_copy(partner, me).start()
            for other in peers:
                @pl.when(other != partner)
                def _():
                    hazard_copy(other, me).start()
        for k in range(per // 2):
            pair_copy(first[i] * (per // 2) + k).start()
        if i == 1:
            hazard_copy(partner, partner).wait_recv()
            block = jnp.sum(hbuf[me - core], axis=0, keepdims=True)
            late = core.astype(jnp.float32)
            factors = [jnp.exp(-late * block), jnp.exp((late - 1.0) * block)]
            factors.append(jnp.zeros((6, paths), jnp.float32))
            pcol[...] = jnp.transpose(jnp.concatenate(factors, axis=0))
        if i >= 1:
            forward(i - 1)

    own_chips = [my_chunk * (per // 2) + lax.rem(lax.rem(chip, per // 2) + k, per // 2) for k in range(per // 2)]
    for q in own_chips[1:]:
        comb[q] = combine(q)
        block_copy(q, chip).start()

    for other in peers:
        @pl.when(other != partner)
        def _():
            hazard_copy(other, other).wait_recv()
    block_sums = jnp.sum(hbuf[...], axis=1)
    before = jnp.zeros((1, paths), jnp.float32)
    prefix = []
    for k in range(n_tm):
        prefix.append(before)
        before = before + block_sums[k : k + 1, :]
    earlier = jnp.exp(-jnp.concatenate(prefix, axis=0))
    erow[...] = earlier
    ecol[...] = jnp.transpose(earlier)
    mine = jnp.broadcast_to(erow[pl.ds(me, 1), :], (8, paths))
    set_part = jnp.dot(
        mine, contrib[...], precision=lax.Precision.HIGHEST, preferred_element_type=jnp.float32
    )
    row_a[...] = set_part[:1] * (1.0 / (paths * n_path))
    for other in peers:
        plane_row(other, me).start()
    rows_a[me] = row_a[...]
    recv[chip] = combine(own_chips[0])

    for other in peers:
        plane_row(other, other).wait_recv()
    row_b[...] = jnp.sum(rows_a[...], axis=0)
    for other in path_peers:
        path_row(other, path_at).start()
    rows_b[path_at] = row_b[...]

    other_chips = [lax.rem(chip + k, chips) for k in range(1, chips)]
    for q in other_chips:
        block_copy(q, q).wait_recv()
    factor = ecol[own_rows(me), :]
    result = None
    for k in range(chips):
        term = factor[:, 2 * k : 2 * k + 1] * recv[k]
        result = term if result is None else result + term
    out[...] = result

    for other in path_peers:
        path_row(other, other).wait_recv()
    sums = jnp.broadcast_to(jnp.sum(rows_b[...], axis=0), (8, SETS))
    share = SETS // n_all
    turned = pltpu.roll(sums, lax.rem(SETS - flat * share, SETS), 1)
    set_out[...] = turned[:1, :share]

    for other in peers:
        hazard_copy(other, me).wait_send()
        plane_row(other, me).wait_send()
    for other in path_peers:
        path_row(other, path_at).wait_send()
    for q in other_chips:
        pair_copy(q).wait_send()
        block_copy(q, chip).wait_send()
    pair_copy(chip).wait_send()


def finish(pathwise, sets, pathwise_out, sets_out):
    pathwise_out[...] = pathwise[...]
    sets_out[...] = sets[...]


def solution(mesh):
    n_path, n_tm = mesh.shape["path"], mesh.shape["tm"]
    n_all = n_path * n_tm

    def on_device(values, hazard, spread, trade_set):
        paths, dates, trades = values.shape
        own = paths // n_tm
        chunks = paths // CHUNK_PATHS
        f32 = jnp.float32
        any_space = pl.BlockSpec(memory_space=pltpu.HBM)
        vmem = pl.BlockSpec(memory_space=pltpu.VMEM)
        dma = pltpu.SemaphoreType.DMA
        pathwise, sets = pl.pallas_call(
            functools.partial(kernel, n_path, n_tm),
            out_shape=(
                jax.ShapeDtypeStruct((own, SETS), f32),
                jax.ShapeDtypeStruct((1, SETS // n_all), f32),
            ),
            in_specs=[any_space, any_space, pl.BlockSpec(memory_space=pltpu.SMEM), any_space],
            out_specs=(vmem, vmem),
            scratch_shapes=[
                pltpu.VMEM((paths * dates, trades), jnp.bfloat16),
                pltpu.VMEM((trades // LANES, LANES), jnp.int32),
                pltpu.VMEM((SETS, trades), jnp.bfloat16),
                pltpu.VMEM((dates, paths), f32),
                pltpu.VMEM((chunks, SETS // LANES, CHUNK_PATHS * dates, LANES), f32),
                pltpu.VMEM((paths, 8), f32),
                pltpu.VMEM((paths, SETS), f32),
                pltpu.VMEM((n_tm // 2, own, SETS), f32),
                pltpu.VMEM((n_tm // 2, own, SETS), f32),
                pltpu.VMEM((n_tm // 2, own, SETS), f32),
                pltpu.VMEM((n_tm, dates, paths), f32),
                pltpu.VMEM((paths, 8), f32),
                pltpu.VMEM((n_tm, paths), f32),
                pltpu.VMEM((paths, n_tm), f32),
                pltpu.VMEM((1, SETS), f32),
                pltpu.VMEM((1, SETS), f32),
                pltpu.VMEM((n_tm, 1, SETS), f32),
                pltpu.VMEM((n_path, 1, SETS), f32),
                dma((chunks,)),
                dma((2,)),
                dma((n_tm,)),
                dma((n_tm,)),
                dma((n_tm // 2,)),
                dma((n_tm // 2,)),
                dma((n_tm // 2,)),
                dma((n_tm // 2,)),
                dma((n_tm,)),
                dma((n_tm,)),
                dma((n_path,)),
                dma((n_path,)),
            ],
            compiler_params=pltpu.CompilerParams(
                collective_id=0, has_side_effects=True, vmem_limit_bytes=62 * 1024 * 1024
            ),
        )(values, hazard, spread, trade_set.reshape(trades // LANES, LANES))
        pathwise, sets = pl.pallas_call(
            finish,
            out_shape=(
                jax.ShapeDtypeStruct(pathwise.shape, f32),
                jax.ShapeDtypeStruct(sets.shape, f32),
            ),
            in_specs=[vmem, vmem],
            out_specs=(vmem, vmem),
        )(pathwise, sets)
        return pathwise, sets.reshape(SETS // n_all)

    in_specs = (P("path", "tm", None), P("tm", "path"), P("tm"), P())
    out_specs = (P(("path", "tm"), None), P(("path", "tm")))
    return jax.shard_map(
        on_device, mesh=mesh, in_specs=in_specs, out_specs=out_specs, check_vma=False
    )
```

time: 21.3 us -> 20.7 us (0.972)
  local copies, waits for them, and re-layouts: 2.59 us -> 0 us
  Pallas kernels: 17.9 us -> 19.8 us
    unnamed x2 -> x0, local copies, waits for them, and re-layouts: 2.59 us -> none
    pallas_call x0 -> x1, Pallas kernels: none -> 1.48 us  [on_device(): pl.pallas_call(finish, out_shape=(jax.ShapeDtypeStruct(pathwise.shape, f3...]
    pallas_call x1, Pallas kernels: 17.9 us -> 18.3 us  [on_device(): pl.pallas_call(functools.partial(kernel, n_path, n_tm), out_shape=(jax.Sh...]
where the time goes in v2:
time: 20.7 us; the launch traced here: 20.4 us
  Pallas kernels  19.8 us (96%)
  between operations  0.64 us (3%)
    pallas_call x1, Pallas kernels, on_device(): pl.pallas_call(functools.partial(kernel, n_path, n_tm), out_shape=(jax.Sh...  18.3 us
    pallas_call x1, Pallas kernels, on_device(): pl.pallas_call(finish, out_shape=(jax.ShapeDtypeStruct(pathwise.shape, f3...  1.48 us

profile of v2, /device:TPU:0, one launch (start us, length us, event | category | flops | bytes accessed | tf_op | source)
XLA Modules:
  0.0 20.4 jit_solution(9708899480811295106)
XLA Ops:
  0.6 18.3 %shard_map.59 = (f32[64,256]{1,0:T(8,128)}, f32[1,8]{1,0:T(1,128)}) custom-call(bf16[512,2,2048]{2,1,0:T(2,128)(2,1)} %values.1, f32[2,512]{1,0:T(2,128)} %hazard_in.1, f32[2]{0:T(128)} %spread.1, s32[16,128]{1,0:T(8,128)} %bitcast.2), custom_call_target="tpu_custom_call" | custom-call | tf_op jit(solution)/shard_map/pallas_call | solution.py:225
  19.0 1.5 %shard_map.60 = (f32[64,256]{1,0:T(8,128)}, f32[1,8]{1,0:T(1,128)}) custom-call(f32[64,256]{1,0:T(8,128)} %get-tuple-element.6.pathwise, f32[1,8]{1,0:T(1,128)} %get-tuple-element.7.sets), custom_call_target="tpu_custom_call" | custom-call | tf_op jit(solution)/shard_map/pallas_call | solution.py:269

commit v3 on v2

--- a/solution.py
+++ b/solution.py
@@ -15,8 +15,8 @@
 
 def kernel(
     n_path, n_tm, values, hazard_in, spread, trade_in, out, set_out,
-    vbuf, ts, oh, hz, nbuf, wt, contrib, pair, comb, recv, hbuf, pcol, erow, ecol, row_a, row_b, rows_a, rows_b,
-    load_sem, small_sem, h_send, h_recv, p_send, p_recv, b_send, b_recv, a_send, a_recv, z_send, z_recv,
+    vbuf, ts, oh, hz, nbuf, wt, contrib, pair, comb, recv, hbuf, pcol, erow, ecol, row_a, rows_a,
+    load_sem, small_sem, h_send, h_recv, p_send, p_recv, b_send, b_recv, a_send, a_recv, ready,
 ):
     paths, dates, trades = values.shape
     own = paths // n_tm
@@ -88,11 +88,11 @@
     def block_copy(q, slot):
         return remote(comb.at[q], recv.at[slot], b_send.at[q], b_recv.at[slot], (path_at, q * 2 + core))
 
-    def plane_row(other, slot):
-        return remote(row_a, rows_a.at[slot], a_send.at[other], a_recv.at[slot], (path_at, other))
-
-    def path_row(other, slot):
-        return remote(row_b, rows_b.at[slot], z_send.at[other], z_recv.at[slot], (other, me))
+    targets = [(z, other) for z in path_peers for other in peers + [me]]
+    targets += [(path_at, other) for other in peers]
+
+    def set_row(z, other, slot):
+        return remote(row_a, rows_a.at[slot], a_send.at[z * n_tm + other], a_recv.at[slot], (z, other))
 
     def combine(q):
         pair_copy(q).wait_recv()
@@ -125,6 +125,8 @@
             contrib[path_span, pl.ds(h * LANES, LANES)] = part
         if i == 0:
             pl.semaphore_wait(barrier, n_tm - 1 + n_path - 1)
+            for other in path_peers:
+                pl.semaphore_signal(ready, inc=1, device_id=(other, me), device_id_type=MESH)
             hazard_copy(partner, me).start()
             for other in peers:
                 @pl.when(other != partner)
@@ -139,13 +141,8 @@
             factors = [jnp.exp(-late * block), jnp.exp((late - 1.0) * block)]
             factors.append(jnp.zeros((6, paths), jnp.float32))
             pcol[...] = jnp.transpose(jnp.concatenate(factors, axis=0))
-        if i >= 1:
+        if 1 <= i < chunks - 1:
             forward(i - 1)
-
-    own_chips = [my_chunk * (per // 2) + lax.rem(lax.rem(chip, per // 2) + k, per // 2) for k in range(per // 2)]
-    for q in own_chips[1:]:
-        comb[q] = combine(q)
-        block_copy(q, chip).start()
 
     for other in peers:
         @pl.when(other != partner)
@@ -165,17 +162,17 @@
         mine, contrib[...], precision=lax.Precision.HIGHEST, preferred_element_type=jnp.float32
     )
     row_a[...] = set_part[:1] * (1.0 / (paths * n_path))
-    for other in peers:
-        plane_row(other, me).start()
-    rows_a[me] = row_a[...]
+    pl.semaphore_wait(ready, n_path - 1)
+    for z, other in targets:
+        set_row(z, other, flat).start()
+    forward(chunks - 2)
+    own_chips = [my_chunk * (per // 2) + lax.rem(lax.rem(chip, per // 2) + k, per // 2) for k in range(per // 2)]
+    for q in own_chips[1:]:
+        comb[q] = combine(q)
+        block_copy(q, chip).start()
+
+    rows_a[flat] = row_a[...]
     recv[chip] = combine(own_chips[0])
-
-    for other in peers:
-        plane_row(other, other).wait_recv()
-    row_b[...] = jnp.sum(rows_a[...], axis=0)
-    for other in path_peers:
-        path_row(other, path_at).start()
-    rows_b[path_at] = row_b[...]
 
     other_chips = [lax.rem(chip + k, chips) for k in range(1, chips)]
     for q in other_chips:
@@ -187,18 +184,17 @@
         result = term if result is None else result + term
     out[...] = result
 
-    for other in path_peers:
-        path_row(other, other).wait_recv()
-    sums = jnp.broadcast_to(jnp.sum(rows_b[...], axis=0), (8, SETS))
+    for z, other in targets:
+        set_row(z, other, z * n_tm + other).wait_recv()
+    sums = jnp.broadcast_to(jnp.sum(rows_a[...], axis=0), (8, SETS))
     share = SETS // n_all
     turned = pltpu.roll(sums, lax.rem(SETS - flat * share, SETS), 1)
     set_out[...] = turned[:1, :share]
 
     for other in peers:
         hazard_copy(other, me).wait_send()
-        plane_row(other, me).wait_send()
-    for other in path_peers:
-        path_row(other, path_at).wait_send()
+    for z, other in targets:
+        set_row(z, other, flat).wait_send()
     for q in other_chips:
         pair_copy(q).wait_send()
         block_copy(q, chip).wait_send()
@@ -246,9 +242,7 @@
                 pltpu.VMEM((n_tm, paths), f32),
                 pltpu.VMEM((paths, n_tm), f32),
                 pltpu.VMEM((1, SETS), f32),
-                pltpu.VMEM((1, SETS), f32),
-                pltpu.VMEM((n_tm, 1, SETS), f32),
-                pltpu.VMEM((n_path, 1, SETS), f32),
+                pltpu.VMEM((n_all, 1, SETS), f32),
                 dma((chunks,)),
                 dma((2,)),
                 dma((n_tm,)),
@@ -257,10 +251,9 @@
                 dma((n_tm // 2,)),
                 dma((n_tm // 2,)),
                 dma((n_tm // 2,)),
-                dma((n_tm,)),
-                dma((n_tm,)),
-                dma((n_path,)),
-                dma((n_path,)),
+                dma((n_all,)),
+                dma((n_all,)),
+                pltpu.SemaphoreType.REGULAR,
             ],
             compiler_params=pltpu.CompilerParams(
                 collective_id=0, has_side_effects=True, vmem_limit_bytes=62 * 1024 * 1024

time: 20.7 us -> 18.5 us (0.89)
  Pallas kernels: 19.8 us -> 17.6 us
    pallas_call x1, Pallas kernels: 18.3 us -> 16.2 us  [on_device(): pl.pallas_call(functools.partial(kernel, n_path, n_tm), out_shape=(jax.Sh...]
where the time goes in v3:
time: 18.5 us; the launch traced here: 18.3 us
  Pallas kernels  17.6 us (95%)
  between operations  0.64 us (3%)
    pallas_call x1, Pallas kernels, on_device(): pl.pallas_call(functools.partial(kernel, n_path, n_tm), out_shape=(jax.Sh...  16.2 us
    pallas_call x1, Pallas kernels, on_device(): pl.pallas_call(finish, out_shape=(jax.ShapeDtypeStruct(pathwise.shape, f3...  1.48 us

profile of v3, /device:TPU:0, one launch (start us, length us, event | category | flops | bytes accessed | tf_op | source)
XLA Modules:
  0.0 18.3 jit_solution(12172590421992659482)
XLA Ops:
  0.6 16.2 %shard_map.59 = (f32[64,256]{1,0:T(8,128)}, f32[1,8]{1,0:T(1,128)}) custom-call(bf16[512,2,2048]{2,1,0:T(2,128)(2,1)} %values.1, f32[2,512]{1,0:T(2,128)} %hazard_in.1, f32[2]{0:T(128)} %spread.1, s32[16,128]{1,0:T(8,128)} %bitcast.2), custom_call_target="tpu_custom_call" | custom-call | tf_op jit(solution)/shard_map/pallas_call | solution.py:221
  16.8 1.5 %shard_map.60 = (f32[64,256]{1,0:T(8,128)}, f32[1,8]{1,0:T(1,128)}) custom-call(f32[64,256]{1,0:T(8,128)} %get-tuple-element.6.pathwise, f32[1,8]{1,0:T(1,128)} %get-tuple-element.7.sets), custom_call_target="tpu_custom_call" | custom-call | tf_op jit(solution)/shard_map/pallas_call | solution.py:262
